TPU v7x, 32 devices: a whole 2x2x4 slice. The times are simulated.
32 devices in a mesh: rows: 4 (over x, core), batch: 8 (over z, y).
Axes of the slice: x: 2, y: 2, z: 4, core: 2. Of those that a mesh axis runs over, the one named last changes fastest.
Arguments:
- features: bfloat16 [96, 8, 32, 512], P('batch', 'rows'), may hold values from -12 to 12
- norm_gain: float32 [512], replicated, may hold values from 0.25 to 1.75
- norm_bias: float32 [512], replicated, may hold values from -2.5 to 2.5
- conv_weight: bfloat16 [4, 4608], replicated, may hold values from -0.09375 to 0.09375
- embed_weight: float32 [16, 1024], replicated, may hold values from -1.5 to 1.5
- embed_bias: float32 [1024], replicated, may hold values from -2.5 to 2.5
- proj_in: bfloat16 [1024, 2048], P('rows'), may hold values from -0.1875 to 0.1875
- proj_in_bias: float32 [2048], replicated, may hold values from -2.5 to 2.5
- proj_out: bfloat16 [2048, 768], P('rows'), may hold values from -0.125 to 0.125
- proj_out_bias: float32 [768], replicated, may hold values from -2.5 to 2.5
- targets: bfloat16 [96, 4, 16, 768], P('batch', 'rows'), may hold values from -6 to 6
Outputs:
- grad_features: bfloat16 [96, 8, 32, 512], P('batch', 'rows')
- grad_conv: float32 [4, 4608], replicated
- grad_gain: float32 [512], replicated
- grad_bias: float32 [512], replicated
- grad_embed: float32 [16, 1024], replicated
All inputs are finite; a program needn't handle non-finite values.
Results may differ from a plain program's by a relative error of at most 0.012.
Values may be sent and summed in bfloat16 or wider, within the bound.
A program may use at most 128 MiB of HBM per device.

v0:
```python
import functools

import jax
import jax.numpy as jnp
from jax import lax
from jax.experimental import pallas as pl
from jax.experimental.pallas import tpu as pltpu
from jax.sharding import PartitionSpec as P

GROUPS = 32
LATENT = 4
PATCH = 2
EPS_NORM = 1e-06
EPS_UNIT = 1e-06
F32 = jnp.float32
BF16 = jnp.bfloat16
NT = (((1,), (1,)), ((), ()))
TN = (((0,), (0,)), ((), ()))


def dot(a, b, dims=(((1,), (0,)), ((), ()))):
    return lax.dot_general(a, b, dims, preferred_element_type=F32)


def split(x, parts):
    out = []
    for _ in range(parts):
        part = x.astype(BF16).astype(F32)
        out.append(part)
        x = x - part
    return out


def exact_dot(x, exact, parts, dims=(((1,), (0,)), ((), ()))):
    rows = x.shape[0]
    full = dot(jnp.concatenate(split(x, parts), axis=0).astype(BF16), exact, dims)
    return sum(full[i * rows : (i + 1) * rows] for i in range(parts))


def kernel(
    images, height, across, n, nb,
    feat, gain, bias, taps, wslice, win, winb, wout, woutb, targ,
    out, conv_o, gain_o, bias_o, emb_o,
    st, st_in, nrm, slope, act, gs_ref, halo, halo_in, ghalo, ghalo_in,
    vpart, v_in, vcat, pout, hact, hslope, gh_ref, a_ref, a_in, fs, fs_in, stat,
    pack, pack_in, piece, piece_in, emb, emb_in, whole, whole_emb,
    s_send, s_recv, v_send, v_recv, x_send, x_recv, b_send, b_recv,
    h_send, h_recv, g_send, g_recv, a_send, a_recv, f_send, f_recv,
    p_send, p_recv, q_send, q_recv, e_send, e_recv, w_send, w_recv, y_send, y_recv,
):
    me = lax.axis_index("rows")
    cells, channels = feat.shape
    area = height * across
    per_group = channels // GROUPS
    members = n * area * per_group
    hidden = win.shape[1]
    share = wout.shape[0]
    tokens = targ.shape[0]
    tok_cols = across // PATCH
    prev, following = lax.rem(me + n - 1, n), lax.rem(me + 1, n)
    sibling = me + 1 - 2 * lax.rem(me, 2)

    def send(src, dst, ss, rs, peer):
        return pltpu.make_async_remote_copy(
            src_ref=src, dst_ref=dst, send_sem=ss, recv_sem=rs,
            device_id={"rows": peer}, device_id_type=pl.DeviceIdType.MESH,
        )

    def spread(src, dst, ss, rs):
        return [
            send(src, dst.at[k - 1], ss.at[k - 1], rs.at[k - 1], lax.rem(me + k, n))
            for k in range(1, n)
        ]

    barrier = pltpu.get_barrier_semaphore()
    for k in range(1, n):
        pl.semaphore_signal(
            barrier, inc=1, device_id={"rows": lax.rem(me + k, n)},
            device_id_type=pl.DeviceIdType.MESH,
        )
    group = lax.axis_index("batch")
    for k in range(1, nb):
        pl.semaphore_signal(
            barrier, inc=1, device_id={"batch": lax.rem(group + k, nb)},
            device_id_type=pl.DeviceIdType.MESH,
        )
    pl.semaphore_wait(barrier, n + nb - 2)

    def slab(owner):
        return pout.at[pl.ds(pl.multiple_of(owner * share, share), share), :]

    own = pl.ds(pl.multiple_of(me * share, share), share)
    cross = [
        send(wout, slab(me), x_send.at[k - 1], x_recv.at[k - 1], lax.rem(me + 2 * k, n))
        for k in range(1, n // 2)
    ]
    beside = [send(wout, slab(me), b_send.at[0], b_recv.at[0], sibling)]
    for copy in cross + beside:
        copy.start()
    pout[own, :] = wout[...]

    st[...] = jnp.zeros_like(st)

    def stats(b, carry):
        x = feat[pl.ds(pl.multiple_of(b * area, area), area), :].astype(F32)
        total = jnp.sum(x, axis=0, keepdims=True)
        centred = x - total / area
        st[0, pl.ds(b, 1), :] = total
        st[1, pl.ds(b, 1), :] = jnp.sum(centred * centred, axis=0, keepdims=True)
        return carry

    lax.fori_loop(0, images, stats, 0)
    stat_copies = spread(st, st_in, s_send, s_recv)
    for copy in stat_copies:
        copy.start()

    vpart[...] = exact_dot(wslice[...], win[...], 2)
    v_copies = spread(vpart, v_in, v_send, v_recv)
    for copy in v_copies:
        copy.start()
    same = (
        lax.broadcasted_iota(jnp.int32, (channels, channels), 0) // per_group
        == lax.broadcasted_iota(jnp.int32, (channels, channels), 1) // per_group
    )
    pool = jnp.where(same, 1.0, 0.0).astype(BF16)

    for copy in stat_copies:
        copy.wait()
    sums = [st[0]] + [st_in[k, 0] for k in range(n - 1)]
    squares = [st[1]] + [st_in[k, 1] for k in range(n - 1)]
    mean = exact_dot(sum(sums), pool, 3) / members
    spread_sq = sum(
        sq + area * jnp.square(total / area - mean) for total, sq in zip(sums, squares)
    )
    variance = exact_dot(spread_sq, pool, 3) / members
    stat[0] = mean
    stat[1] = lax.rsqrt(variance + EPS_NORM)

    def forward(b, carry):
        where = pl.ds(pl.multiple_of(b * area, area), area)
        x = feat[where, :].astype(F32)
        normed = (x - stat[0, pl.ds(b, 1), :]) * stat[1, pl.ds(b, 1), :]
        shifted = normed * gain[...] + bias[...]
        sig = jax.nn.sigmoid(shifted)
        nrm[where, :] = normed
        act[where, :] = (shifted * sig).astype(BF16)
        slope[where, :] = sig * (1.0 + shifted * (1.0 - sig))
        return carry

    lax.fori_loop(0, images, forward, 0)

    lane = lax.broadcasted_iota(jnp.int32, (8, cells), 1)
    col = lax.rem(lane, across)
    row = lax.rem(lane // across, height)

    def ahead(x, count):
        return pltpu.roll(x, (-count) % cells, 1) if count % cells else x

    def beside_col(x, off):
        if off == 0:
            return x
        ok = (col + off >= 0) & (col + off < across)
        return jnp.where(ok, ahead(x, off), 0.0)

    def above(x, arrived):
        edge = jnp.where(me > 0, ahead(arrived, (height - 1) * across), 0.0)
        return jnp.where(row == 0, edge, ahead(x, -across))

    def below(x, arrived):
        edge = jnp.where(me < n - 1, ahead(arrived, -(height - 1) * across), 0.0)
        return jnp.where(row == height - 1, edge, ahead(x, across))

    terms = dot(taps[...], act[...], NT)
    rows3 = []
    for dy in range(3):
        rows3.append(
            sum(
                beside_col(terms[(3 * dy + dx) * 8 : (3 * dy + dx + 1) * 8], dx - 1)
                for dx in range(3)
            )
        )
    halo[0] = rows3[0]
    halo[1] = rows3[2]
    halo_copies = [
        send(halo.at[0], halo_in.at[0], h_send.at[0], h_recv.at[0], following),
        send(halo.at[1], halo_in.at[1], h_send.at[1], h_recv.at[1], prev),
    ]
    for copy in halo_copies:
        copy.start()
    cell = lax.broadcasted_iota(jnp.int32, (cells, tokens), 0)
    tok = lax.broadcasted_iota(jnp.int32, (cells, tokens), 1)
    per_image = (height // PATCH) * tok_cols
    corner = (
        (tok // per_image) * area
        + (lax.rem(tok, per_image) // tok_cols) * (PATCH * across)
        + lax.rem(tok, tok_cols) * PATCH
    )
    away = cell - corner
    pick = [
        jnp.where(away == u * across + v, 1.0, 0.0).astype(BF16)
        for u in range(PATCH) for v in range(PATCH)
    ]
    for copy in v_copies:
        copy.wait()
    v_all = vpart[...] + sum(v_in[k] for k in range(n - 1))
    inner = PATCH * PATCH * LATENT
    v_hi, v_lo = split(v_all[0:inner], 2)
    vcat[...] = jnp.concatenate([v_hi, v_hi, v_lo], axis=0).astype(BF16)
    pre_bias = v_all[inner : inner + 1] + winb[...]
    for copy in halo_copies:
        copy.wait()
    latent = rows3[1] + above(rows3[0], halo_in[0]) + below(rows3[2], halo_in[1])
    first_half = lax.broadcasted_iota(jnp.int32, (8, tokens), 0) < LATENT
    blocks = []
    for u in range(PATCH):
        pair = [exact_dot(latent, pick[u * PATCH + v], 3) for v in range(PATCH)]
        blocks.append(jnp.where(first_half, pair[0], pair[1]))
    patches = jnp.concatenate(blocks, axis=0)
    p_hi, p_lo = split(patches, 2)
    pcat = jnp.concatenate([p_hi, p_lo, p_hi], axis=0).astype(BF16)

    for copy in cross:
        copy.wait()
    relay = []
    for k in range(1, n // 2):
        owner = lax.rem(me + n - 2 * k, n)
        relay.append(send(slab(owner), slab(owner), b_send.at[k], b_recv.at[k], sibling))
    for copy in relay:
        copy.start()

    step = hidden // 4
    for c in range(4):
        where = slice(c * step, (c + 1) * step)
        pre = dot(pcat, vcat[:, where], TN) + pre_bias[:, where]
        sig = jax.nn.sigmoid(pre)
        hact[:, where] = (pre * sig).astype(BF16)
        hslope[:, where] = sig * (1.0 + pre * (1.0 - sig))
    target = targ[...].astype(F32)
    unit_target = target * lax.rsqrt(jnp.sum(target * target, axis=1, keepdims=True) + EPS_UNIT)
    for copy in beside + relay:
        copy.wait()
    projected = dot(hact[...], pout[...]) + woutb[...]
    inv_len = lax.rsqrt(jnp.sum(projected * projected, axis=1, keepdims=True) + EPS_UNIT)
    unit_proj = projected * inv_len
    cosine = jnp.sum(unit_proj * unit_target, axis=1, keepdims=True)
    grad_out = (-inv_len * (unit_target - cosine * unit_proj)).astype(BF16)
    for c in range(4):
        where = slice(c * step, (c + 1) * step)
        back = dot(grad_out, pout[where, :], NT)
        gh_ref[:, where] = (back * hslope[:, where]).astype(BF16)
    two = dot(vcat[inner:, :], gh_ref[...], NT)
    grad_patch = (two[0:inner] + two[inner:]).astype(BF16)

    grid = []
    for v in range(PATCH):
        grid.append(
            sum(
                dot(grad_patch[u * 8 : (u + 1) * 8], pick[u * PATCH + v], NT)
                for u in range(PATCH)
            )
        )
    low_rows = lax.broadcasted_iota(jnp.int32, (8, cells), 0) < LATENT
    both = jnp.where(low_rows, grid[0], grid[1])
    grad_lat = both + pltpu.roll(both, LATENT, 0)
    grad_lat = jnp.where(low_rows, grad_lat, 0.0)
    ghalo[...] = grad_lat
    ghalo_copies = [
        send(ghalo, ghalo_in.at[0], g_send.at[0], g_recv.at[0], following),
        send(ghalo, ghalo_in.at[1], g_send.at[1], g_recv.at[1], prev),
    ]
    for copy in ghalo_copies:
        copy.start()
    wide = dot(pcat[0 : 2 * inner], gh_ref[...])
    a_ref[...] = wide[0:inner] + wide[inner:]
    a_copies = spread(a_ref, a_in, a_send, a_recv)
    for copy in a_copies:
        copy.start()
    for copy in ghalo_copies:
        copy.wait()
    by_row = [below(grad_lat, ghalo_in[1]), grad_lat, above(grad_lat, ghalo_in[0])]
    grad_taps = jnp.concatenate(
        [beside_col(by_row[dy], 1 - dx) for dy in range(3) for dx in range(3)], axis=0
    ).astype(BF16)
    gs_ref[...] = dot(grad_taps, taps[...], TN)
    fs[...] = jnp.zeros_like(fs)

    def backward(b, carry):
        where = pl.ds(pl.multiple_of(b * area, area), area)
        gs = gs_ref[where, :] * slope[where, :]
        gs_ref[where, :] = gs
        fs[0, pl.ds(b, 1), :] = jnp.sum(gs, axis=0, keepdims=True)
        fs[1, pl.ds(b, 1), :] = jnp.sum(gs * nrm[where, :], axis=0, keepdims=True)
        return carry

    lax.fori_loop(0, images, backward, 0)
    f_copies = spread(fs, fs_in, f_send, f_recv)
    for copy in f_copies:
        copy.start()
    conv = dot(grad_taps, act[...])
    gain_row = jnp.sum(fs[1], axis=0, keepdims=True)
    bias_row = jnp.sum(fs[0], axis=0, keepdims=True)
    row8 = lax.broadcasted_iota(jnp.int32, (8, channels), 0)
    per = pack.shape[1] // 8
    lanes = pack.shape[2]
    for i in range(5):
        block = conv[16 * i : 16 * i + 8]
        if i < 4:
            block = block + pltpu.roll(conv[16 * i + 8 : 16 * i + 16], LATENT, 0)
        else:
            block = jnp.where(row8 == LATENT, gain_row, block)
            block = jnp.where(row8 == LATENT + 1, bias_row, block)
        for c in range(channels // lanes):
            t = 5 * c + i
            pack[t // per, (t % per) * 8 : (t % per + 1) * 8, :] = (
                block[:, c * lanes : (c + 1) * lanes]
            )
    for t in range(5 * (channels // lanes), n * per):
        pack[t // per, (t % per) * 8 : (t % per + 1) * 8, :] = jnp.zeros((8, lanes), F32)
    p_copies = []
    for k in range(1, n):
        peer = lax.rem(me + k, n)
        p_copies.append(
            send(pack.at[peer], pack_in.at[k - 1], p_send.at[k - 1], p_recv.at[k - 1], peer)
        )
    for copy in p_copies:
        copy.start()
    for copy in a_copies:
        copy.wait()
    a_all = a_ref[...] + sum(a_in[k] for k in range(n - 1))
    emb[...] = exact_dot(a_all, win[...], 2, NT)

    def across_batch(src, dst, ss, rs):
        return [
            pltpu.make_async_remote_copy(
                src_ref=src, dst_ref=dst.at[k - 1], send_sem=ss.at[k - 1], recv_sem=rs.at[k - 1],
                device_id={"batch": lax.rem(group + k, nb)}, device_id_type=pl.DeviceIdType.MESH,
            )
            for k in range(1, nb)
        ]

    q_copies = across_batch(emb, emb_in, e_send, e_recv)
    for copy in q_copies:
        copy.start()
    for copy in p_copies:
        copy.wait()
    piece[...] = pack[me] + sum(pack_in[k] for k in range(n - 1))
    piece_copies = across_batch(piece, piece_in, q_send, q_recv)
    for copy in piece_copies:
        copy.start()
    for copy in f_copies:
        copy.wait()
    for i in range(2):
        total = (fs[i] + sum(fs_in[k, i] for k in range(n - 1))) * gain[...]
        stat_i = exact_dot(total, pool, 3) / members
        stat[2 + i] = stat_i

    def finish(b, carry):
        where = pl.ds(pl.multiple_of(b * area, area), area)
        one = pl.ds(b, 1)
        out[where, :] = (
            stat[1, one, :]
            * (gs_ref[where, :] * gain[...] - stat[2, one, :] - nrm[where, :] * stat[3, one, :])
        ).astype(BF16)
        return carry

    lax.fori_loop(0, images // 2, finish, 0)
    for copy in q_copies + piece_copies:
        copy.wait()
    whole[me] = ordered(piece, piece_in, group, nb)
    whole_emb[me] = ordered(emb, emb_in, group, nb)
    w_copies = []
    for k in range(1, n):
        peer = lax.rem(me + k, n)
        w_copies.append(send(whole.at[me], whole.at[me], w_send.at[k - 1], w_recv.at[k - 1], peer))
        w_copies.append(
            send(whole_emb.at[me], whole_emb.at[me], y_send.at[k - 1], y_recv.at[k - 1], peer)
        )
    for copy in w_copies:
        copy.start()
    lax.fori_loop(images // 2, images, finish, 0)
    for copy in w_copies:
        copy.wait()
    for c in range(channels // lanes):
        at = slice(c * lanes, (c + 1) * lanes)
        for i in range(5):
            t = 5 * c + i
            tile = whole[t // per, (t % per) * 8 : (t % per + 1) * 8, :]
            for half in range(2):
                tap = 2 * i + half
                rows = tile[half * LATENT : (half + 1) * LATENT]
                if tap < 9:
                    start = tap * channels + c * lanes
                    conv_o[:, start : start + lanes] = rows
                else:
                    gain_o[:, at] = rows[0:1]
                    bias_o[:, at] = rows[1:2]
    part = emb.shape[1]
    for k in range(n):
        emb_o[:, k * part : (k + 1) * part] = whole_emb[k]


def ordered(own, arrived, group, nb):
    total = None
    for g in range(nb):
        slot = lax.rem(group + nb - g, nb)
        value = arrived[jnp.maximum(slot - 1, 0)] if nb > 1 else own[...]
        value = jnp.where(slot == 0, own[...], value)
        total = value if total is None else total + value
    return total


def shards(
    features, norm_gain, norm_bias, conv_weight, embed_weight, embed_bias,
    proj_in, proj_in_bias, proj_out, proj_out_bias, targets,
):
    images, height, across, channels = features.shape
    n = lax.axis_size("rows")
    nb = lax.axis_size("batch")
    lanes = 128
    per = -(-(5 * (channels // lanes)) // n)
    me = lax.axis_index("rows")
    cells = images * height * across
    align = targets.shape[-1]
    tokens = targets.shape[0] * targets.shape[1] * targets.shape[2]
    inner, width = embed_weight.shape
    part, hidden = proj_in.shape
    share = proj_out.shape[0]
    pad_images = -(-images // 8) * 8
    taps = conv_weight.reshape(LATENT, 9, channels).transpose(1, 0, 2)
    taps = jnp.concatenate([taps, taps], axis=1).reshape(72, channels)
    wide = jnp.concatenate(
        [embed_weight, embed_bias[None], jnp.zeros((7, width), F32)], axis=0
    )
    wslice = lax.dynamic_slice_in_dim(wide, me * part, part, axis=1)
    rows = wslice.shape[0]
    dma = pltpu.SemaphoreType.DMA
    chips = max(n // 2 - 1, 1)
    vm = pltpu.VMEM
    grad_features, grad_conv, grad_gain, grad_bias, grad_embed = pl.pallas_call(
        functools.partial(kernel, images, height, across, n, nb),
        out_shape=(
            jax.ShapeDtypeStruct((cells, channels), BF16),
            jax.ShapeDtypeStruct((LATENT, 9 * channels), F32),
            jax.ShapeDtypeStruct((1, channels), F32),
            jax.ShapeDtypeStruct((1, channels), F32),
            jax.ShapeDtypeStruct((inner, width), F32),
        ),
        in_specs=[pl.BlockSpec(memory_space=vm)] * 10,
        out_specs=[pl.BlockSpec(memory_space=vm)] * 5,
        scratch_shapes=[
            vm((2, pad_images, channels), F32),
            vm((n - 1, 2, pad_images, channels), F32),
            vm((cells, channels), F32),
            vm((cells, channels), F32),
            vm((cells, channels), BF16),
            vm((cells, channels), F32),
            vm((2, 8, cells), F32),
            vm((2, 8, cells), F32),
            vm((8, cells), F32),
            vm((2, 8, cells), F32),
            vm((rows, hidden), F32),
            vm((n - 1, rows, hidden), F32),
            vm((3 * inner, hidden), BF16),
            vm((n * share, align), BF16),
            vm((tokens, hidden), BF16),
            vm((tokens, hidden), F32),
            vm((tokens, hidden), BF16),
            vm((inner, hidden), F32),
            vm((n - 1, inner, hidden), F32),
            vm((2, pad_images, channels), F32),
            vm((n - 1, 2, pad_images, channels), F32),
            vm((4, pad_images, channels), F32),
            vm((n, per * 8, lanes), F32),
            vm((n - 1, per * 8, lanes), F32),
            vm((per * 8, lanes), F32),
            vm((max(nb - 1, 1), per * 8, lanes), F32),
            vm((inner, part), F32),
            vm((max(nb - 1, 1), inner, part), F32),
            vm((n, per * 8, lanes), F32),
            vm((n, inner, part), F32),
            dma((n - 1,)), dma((n - 1,)), dma((n - 1,)), dma((n - 1,)),
            dma((chips,)), dma((chips,)), dma((chips + 1,)), dma((chips + 1,)),
            dma((2,)), dma((2,)), dma((2,)), dma((2,)),
            dma((n - 1,)), dma((n - 1,)), dma((n - 1,)), dma((n - 1,)),
            dma((n - 1,)), dma((n - 1,)),
            dma((max(nb - 1, 1),)), dma((max(nb - 1, 1),)),
            dma((max(nb - 1, 1),)), dma((max(nb - 1, 1),)),
            dma((n - 1,)), dma((n - 1,)), dma((n - 1,)), dma((n - 1,)),
        ],
        compiler_params=pltpu.CompilerParams(
            collective_id=0, has_side_effects=True, vmem_limit_bytes=60 * 1024 * 1024
        ),
        name="alignment_step",
    )(
        features.reshape(cells, channels), norm_gain[None], norm_bias[None], taps, wslice,
        proj_in, proj_in_bias[None], proj_out, proj_out_bias[None],
        targets.reshape(tokens, align),
    )
    return (
        grad_features.reshape(images, height, across, channels),
        grad_conv, grad_gain[0], grad_bias[0], grad_embed,
    )


def solution(mesh):
    in_specs = (
        P("batch", "rows", None, None), P(), P(), P(), P(), P(),
        P("rows", None), P(), P("rows", None), P(), P("batch", "rows", None, None),
    )
    out_specs = (P("batch", "rows", None, None), P(), P(), P(), P())
    return jax.shard_map(shards, mesh=mesh, in_specs=in_specs, out_specs=out_specs, check_vma=False)
```

profile of v0, /device:TPU:0, one launch (start us, length us, event | category | flops | bytes accessed | tf_op | source)
XLA Modules:
  0.0 73.4 jit_solution(2340195772735616786)
XLA Ops:
  0.6 0.0 copy-start.4
  0.7 0.0 copy-start.3
  0.7 0.1 pad.2.clone
  0.7 0.6 copy-done.4
  1.3 0.6 broadcast_in_dim.23.woutb
  1.9 0.0 copy-done.3
  1.9 0.0 copy-start.2
  1.9 1.4 %fusion.1.wslice = f32[24,256]{1,0:T(8,128)} fusion(s32[]{:T(128)S(6)} %select_n.3, f32[16,1024]{1,0:T(8,128)} %param.15, f32[1,1024]{1,0:T(1,128)S(1)} %bitcast.19, f32[24]{0:T(128)S(1)} %pad.2.clone), kind=kLoop, calls=%fused_computation.5 | loop fusion | flops 12288 | bytes 94308 | tf_op jit(solution)/shard_map/concatenate | solution.py:431
  3.3 0.0 copy-done.2
  3.4 0.7 copy.19
  4.0 64.6 %alignment_step.1 = (bf16[768,512]{1,0:T(8,128)(2,1)}, f32[4,4608]{1,0:T(4,128)}, f32[1,512]{1,0:T(1,128)}, f32[1,512]{1,0:T(1,128)}, f32[16,1024]{1,0:T(8,128)}) custom-call(bf16[768,512]{1,0:T(8,128)(2,1)} %bitcast.14, f32[1,512]{1,0:T(1,128)} %bitcast.20, f32[1,512]{1,0:T(1,128)} %bitcast.21, bf16[72,512]{1,0:T(8,128)(2,1)} %bitcast.16, ...), custom_call_target="tpu_custom_call" | custom-call | tf_op jit(solution)/shard_map/alignment_step/pallas_call | solution.py:439
  68.7 0.0 copy-start
  68.7 2.1 %copy.25 = bf16[12,2,32,512]{3,2,1,0:T(8,128)(2,1)} copy(bf16[12,2,32,512]{3,2,1,0:T(8,128)(2,1)} %bitcast.13) | data formatting | bytes 1572864
  70.8 0.0 copy-done
  70.8 0.0 copy-start.6
  70.8 0.0 copy-start.1
  70.8 0.6 copy.26
  71.5 0.0 copy-done.6
  71.5 0.0 copy-start.5
  71.5 0.6 copy.27
  72.1 0.1 copy-done.5
  72.2 0.6 copy.28
  72.7 0.0 copy-done.1
  72.7 0.6 copy.29
  (3 shorter events, 0.0 us)
Async XLA Ops:
  0.6 0.7 copy-start.4
  0.7 1.3 %copy-start.3 = (f32[1024]{0:T(1024)S(1)}, f32[1024]{0:T(1024)}, u32[]{:S(2)}) copy-start(f32[1024]{0:T(1024)} %param.16) | copy-start | bytes 12292
  1.9 1.4 %copy-start.2 = (bf16[4,4608]{1,0:T(4,128)(2,1)S(1)}, bf16[4,4608]{1,0:T(4,128)(2,1)}, u32[]{:S(2)}) copy-start(bf16[4,4608]{1,0:T(4,128)(2,1)} %param.14) | copy-start | bytes 110596
  68.7 2.1 %copy-start = (f32[4,4608]{1,0:T(4,128)S(1)}, f32[4,4608]{1,0:T(4,128)}, u32[]{:S(2)}) copy-start(f32[4,4608]{1,0:T(4,128)} %get-tuple-element.21) | copy-start | bytes 221188
  70.8 0.7 copy-start.6
  70.8 1.9 %copy-start.1 = (f32[16,1024]{1,0:T(8,128)S(1)}, f32[16,1024]{1,0:T(8,128)}, u32[]{:S(2)}) copy-start(f32[16,1024]{1,0:T(8,128)} %get-tuple-element.24) | copy-start | bytes 196612
  71.5 0.7 copy-start.5
where the time goes:
time: 73.7 us; the launch traced here: 73.4 us
  Pallas kernels  64.6 us (88%)
  local copies, waits for them, and re-layouts  6.62 us (9%)
  other arithmetic  1.42 us (2%)
    pallas_call x1, Pallas kernels, shards(): pl.pallas_call(functools.partial(kernel, images, height, across, n, nb),...  64.6 us
    unnamed x19, local copies, waits for them, and re-layouts  5.26 us

commit v1 on v0

v1 whole, which is shorter than its diff:
```python
import functools

import jax
import jax.numpy as jnp
from jax import lax
from jax.experimental import pallas as pl
from jax.experimental.pallas import tpu as pltpu
from jax.sharding import PartitionSpec as P

GROUPS = 32
LATENT = 4
PATCH = 2
EPS_NORM = 1e-06
EPS_UNIT = 1e-06
F32 = jnp.float32
BF16 = jnp.bfloat16
NT = (((1,), (1,)), ((), ()))
TN = (((0,), (0,)), ((), ()))


def dot(a, b, dims=(((1,), (0,)), ((), ()))):
    return lax.dot_general(a, b, dims, preferred_element_type=F32)


def split(x, parts):
    out = []
    for _ in range(parts):
        part = x.astype(BF16).astype(F32)
        out.append(part)
        x = x - part
    return out


def exact_dot(x, exact, parts, dims=(((1,), (0,)), ((), ()))):
    rows = x.shape[0]
    full = dot(jnp.concatenate(split(x, parts), axis=0).astype(BF16), exact, dims)
    return sum(full[i * rows : (i + 1) * rows] for i in range(parts))


def kernel(
    images, height, across, n, nb, sliced,
    feat_h, gain_h, bias_h, conv_h, embw_h, embb_h, win_h, winb_h, wout_h, woutb_h, targ_h,
    out, conv_o, gain_o, bias_o, emb_o,
    feat, gain, bias, cw, we, web, win, winb, woutb, targ,
    st, sg, sg_in, nrm, slope, act, gs_ref, halo, halo_in, ghalo, ghalo_in,
    vpart, v1_in, vhalf, vs16, v2_in, vfull, vcat, pout, hact, hslope, gh_ref,
    a_ref, a16, a_in, fs, fg, fg_in, stat,
    pack, pack_in, piece, piece_in, emb, emb_in, whole, whole_emb,
    l_sem, s_send, s_recv, v_send, v_recv, x_send, x_recv,
    h_send, h_recv, g_send, g_recv, a_send, a_recv, f_send, f_recv,
    p_send, p_recv, q_send, q_recv, e_send, e_recv, w_send, w_recv, y_send, y_recv,
):
    me = lax.axis_index("rows")
    group = lax.axis_index("batch")
    cells, channels = feat.shape
    area = height * across
    per_group = channels // GROUPS
    members = n * area * per_group
    hidden = win.shape[1]
    part = win.shape[0]
    share = wout_h.shape[0]
    tokens = targ.shape[0]
    tok_cols = across // PATCH
    prev, following = lax.rem(me + n - 1, n), lax.rem(me + 1, n)
    odd = lax.rem(me, 2)
    sibling = me + 1 - 2 * odd
    sent = []

    def to(src, dst, ss, rs, where):
        copy = pltpu.make_async_remote_copy(
            src_ref=src, dst_ref=dst, send_sem=ss, recv_sem=rs,
            device_id=where, device_id_type=pl.DeviceIdType.MESH,
        )
        copy.start()
        sent.append(copy)
        return copy

    def send(src, dst, ss, rs, peer):
        return to(src, dst, ss, rs, {"rows": peer})

    def spread(src, dst, ss, rs):
        return [
            send(src, dst.at[k - 1], ss.at[k - 1], rs.at[k - 1], lax.rem(me + k, n))
            for k in range(1, n)
        ]

    def across_batch(src, dst, ss, rs):
        return [
            to(src, dst.at[k - 1], ss.at[k - 1], rs.at[k - 1], {"batch": lax.rem(group + k, nb)})
            for k in range(1, nb)
        ]

    def arrive(copies):
        for copy in copies:
            copy.wait_recv()

    barrier = pltpu.get_barrier_semaphore()
    for k in range(1, n):
        pl.semaphore_signal(
            barrier, inc=1, device_id={"rows": lax.rem(me + k, n)},
            device_id_type=pl.DeviceIdType.MESH,
        )
    for k in range(1, nb):
        pl.semaphore_signal(
            barrier, inc=1, device_id={"batch": lax.rem(group + k, nb)},
            device_id_type=pl.DeviceIdType.MESH,
        )

    def slab(owner):
        return pl.ds(pl.multiple_of(owner * share, share), share)

    if sliced:
        cols = pl.ds(pl.multiple_of(me * part, part), part)
        embw_v, embb_v = embw_h.at[:, cols], embb_h.at[:, cols]
    else:
        embw_v, embb_v = embw_h, embb_h
    loads = [
        pltpu.make_async_copy(src, dst, l_sem.at[i])
        for i, (src, dst) in enumerate([
            (feat_h, feat), (embw_v, we), (embb_v, web), (win_h, win),
            (wout_h, pout.at[slab(me), :]), (conv_h, cw), (gain_h, gain), (bias_h, bias),
            (winb_h, winb), (woutb_h, woutb), (targ_h, targ),
        ])
    ]
    for load in loads:
        load.start()

    st[...] = jnp.zeros_like(st)
    fs[...] = jnp.zeros_like(fs)
    pool = jnp.where(
        lax.broadcasted_iota(jnp.int32, (channels, 128), 0) // per_group
        == lax.broadcasted_iota(jnp.int32, (channels, 128), 1),
        1.0, 0.0,
    ).astype(BF16)
    loads[0].wait()

    def stats(b, carry):
        x = feat[pl.ds(pl.multiple_of(b * area, area), area), :].astype(F32)
        total = jnp.sum(x, axis=0, keepdims=True)
        centred = x - total / area
        st[0, pl.ds(b, 1), :] = total
        st[1, pl.ds(b, 1), :] = jnp.sum(centred * centred, axis=0, keepdims=True)
        return carry

    lax.fori_loop(0, images, stats, 0)
    count = area * per_group
    group_total = exact_dot(st[0], pool, 3)
    local_mean = exact_dot(group_total / count, pool, 3, NT)
    sg[0] = group_total
    sg[1] = exact_dot(st[1] + area * jnp.square(st[0] / area - local_mean), pool, 3)

    for load in loads[1:4]:
        load.wait()
    first_row = lax.broadcasted_iota(jnp.int32, (8, part), 0) == 0
    wcat = jnp.concatenate([we[...], jnp.where(first_row, web[...], 0.0)], axis=0)
    vpart[...] = exact_dot(wcat, win[...], 2)
    for load in loads[4:]:
        load.wait()
    pl.semaphore_wait(barrier, n + nb - 2)

    half = hidden // 2
    mine = pl.ds(pl.multiple_of(odd * half, half), half)
    theirs = pl.ds(pl.multiple_of((1 - odd) * half, half), half)
    v1 = send(vpart.at[:, theirs], v1_in, v_send.at[0], v_recv.at[0], sibling)
    stat_copies = spread(sg, sg_in, s_send, s_recv)

    quarter = share // 4
    fine = quarter // 4 if (quarter // 4) % 16 == 0 else quarter // 2
    parts = {
        "a": (0, quarter // 2), "b1": (quarter // 2, fine), "b2": (quarter // 2 + fine, quarter // 2 - fine),
        "d": (quarter // 2, quarter // 2), "e1": (0, fine), "e2": (fine, quarter // 2 - fine),
    }
    q0 = lax.rem(group, 4)
    q1 = q0 + 1 - 2 * lax.rem(q0, 2)
    q2 = lax.rem(q0 + 2, 4)
    q3 = lax.rem(q1 + 2, 4)
    y_peer = {"batch": group + 1 - 2 * lax.rem(group, 2)}
    z_peer = {"batch": group - q0 + q2}
    ring = n // 2 - 1
    names = [
        ("x", "a", q0), ("x", "b1", q0), ("x", "b2", q0), ("x", "d", q3),
        ("y", "a", q1), ("y", "b1", q1), ("y", "b2", q1), ("y", "e2", q3),
        ("z", "a", q2), ("z", "b1", q2), ("z", "b2", q2), ("z", "e1", q3),
    ]
    names = [item for item in names if parts[item[1]][1]]
    slot = {(link, name): i for i, (link, name, _) in enumerate(names)}
    arriving = {}
    relays = []

    def block(owner, q, name):
        start, size = parts[name]
        unit = min(size, fine)
        return pout.at[pl.ds(pl.multiple_of(owner * share + q * quarter + start, unit), size), :]

    def owner_of(k):
        return lax.rem(me + n - 2 * k, n)

    def push(link, name, k, owner, q, where):
        if not parts[name][1]:
            return
        i = (k - 1) * 2 * len(names) + slot[link, name]
        ref = block(owner, q, name)
        arriving[link, name, k] = to(ref, ref, x_send.at[i], x_recv.at[i], where)

    def over_x(name):
        for k in range(1, ring + 1):
            push("x", name, k, me, q3 if name == "d" else q0, {"rows": lax.rem(me + 2 * k, n)})

    def relay(link, name, onward=()):
        q = {item[:2]: item[2] for item in names}
        for k in range(1, ring + 1):
            if (link, name, k) not in arriving:
                continue
            arriving[link, name, k].wait_recv()
            for next_link, next_name in onward:
                push(
                    next_link, next_name, k, owner_of(k), q[link, name],
                    y_peer if next_link == "y" else z_peer,
                )
            i = ((k - 1) * 2 + 1) * len(names) + slot[link, name]
            ref = block(owner_of(k), q[link, name], name)
            relays.append(to(ref, ref, x_send.at[i], x_recv.at[i], {"rows": sibling}))

    over_x("a")
    last = 2 * ring * len(names)
    own = pout.at[slab(me), :]
    beside = send(own, own, x_send.at[last], x_recv.at[last], sibling)

    v1.wait_recv()
    v_half = vpart[:, mine] + v1_in[...]
    vhalf[...] = v_half
    vs16[...] = v_half.astype(BF16)
    v2 = [
        send(vs16, v2_in.at[k - 1], v_send.at[k], v_recv.at[k], lax.rem(me + 2 * k, n))
        for k in range(1, ring + 1)
    ]
    over_x("b1")

    weights = cw[...].astype(F32)
    weights = jnp.concatenate([weights, weights], axis=0)
    taps = jnp.concatenate(
        [weights[:, t * channels : (t + 1) * channels] for t in range(9)], axis=0
    ).astype(BF16)

    arrive(stat_copies)
    sums = [sg[0]] + [sg_in[k, 0] for k in range(n - 1)]
    squares = [sg[1]] + [sg_in[k, 1] for k in range(n - 1)]
    mean = sum(sums) / members
    variance = sum(
        sq + count * jnp.square(total / count - mean) for total, sq in zip(sums, squares)
    ) / members
    rows = mean.shape[0]
    both_stats = exact_dot(
        jnp.concatenate([mean, lax.rsqrt(variance + EPS_NORM)], axis=0), pool, 3, NT
    )
    stat[0] = both_stats[0:rows]
    stat[1] = both_stats[rows:]

    def forward(b, carry):
        where = pl.ds(pl.multiple_of(b * area, area), area)
        x = feat[where, :].astype(F32)
        normed = (x - stat[0, pl.ds(b, 1), :]) * stat[1, pl.ds(b, 1), :]
        shifted = normed * gain[...] + bias[...]
        sig = jax.nn.sigmoid(shifted)
        nrm[where, :] = normed
        act[where, :] = (shifted * sig).astype(BF16)
        slope[where, :] = sig * (1.0 + shifted * (1.0 - sig))
        return carry

    lax.fori_loop(0, images, forward, 0)

    lane = lax.broadcasted_iota(jnp.int32, (8, cells), 1)
    col = lax.rem(lane, across)
    row = lax.rem(lane // across, height)

    def ahead(x, count):
        return pltpu.roll(x, (-count) % cells, 1) if count % cells else x

    def beside_col(x, off):
        if off == 0:
            return x
        ok = (col + off >= 0) & (col + off < across)
        return jnp.where(ok, ahead(x, off), 0.0)

    def above(x, arrived):
        edge = jnp.where(me > 0, ahead(arrived, (height - 1) * across), 0.0)
        return jnp.where(row == 0, edge, ahead(x, -across))

    def below(x, arrived):
        edge = jnp.where(me < n - 1, ahead(arrived, -(height - 1) * across), 0.0)
        return jnp.where(row == height - 1, edge, ahead(x, across))

    terms = dot(taps, act[...], NT)
    rows3 = []
    for dy in range(3):
        rows3.append(
            sum(
                beside_col(terms[(3 * dy + dx) * 8 : (3 * dy + dx + 1) * 8], dx - 1)
                for dx in range(3)
            )
        )
    halo[0] = rows3[0]
    halo[1] = rows3[2]
    halo_copies = [
        send(halo.at[0], halo_in.at[0], h_send.at[0], h_recv.at[0], following),
        send(halo.at[1], halo_in.at[1], h_send.at[1], h_recv.at[1], prev),
    ]
    over_x("b2")
    over_x("d")
    relay("x", "a", (("y", "a"), ("z", "a")))
    cell = lax.broadcasted_iota(jnp.int32, (cells, tokens), 0)
    tok = lax.broadcasted_iota(jnp.int32, (cells, tokens), 1)
    per_image = (height // PATCH) * tok_cols
    corner = (
        (tok // per_image) * area
        + (lax.rem(tok, per_image) // tok_cols) * (PATCH * across)
        + lax.rem(tok, tok_cols) * PATCH
    )
    away = cell - corner
    pick = [
        jnp.where(away == u * across + v, 1.0, 0.0).astype(BF16)
        for u in range(PATCH) for v in range(PATCH)
    ]
    arrive(v2)
    vfull[:, mine] = vhalf[...] + sum(v2_in[k].astype(F32) for k in range(ring))
    v3 = send(vfull.at[:, mine], vfull.at[:, mine], v_send.at[ring + 1], v_recv.at[ring + 1], sibling)
    arrive(halo_copies)
    relay("x", "b1", (("y", "b1"), ("z", "b1")))
    inner = PATCH * PATCH * LATENT
    latent = rows3[1] + above(rows3[0], halo_in[0]) + below(rows3[2], halo_in[1])
    first_half = lax.broadcasted_iota(jnp.int32, (8, tokens), 0) < LATENT
    blocks = []
    for u in range(PATCH):
        pair = [exact_dot(latent, pick[u * PATCH + v], 3) for v in range(PATCH)]
        blocks.append(jnp.where(first_half, pair[0], pair[1]))
    patches = jnp.concatenate(blocks, axis=0)
    p_hi, p_lo = split(patches, 2)
    pcat = jnp.concatenate([p_hi, p_lo, p_hi], axis=0).astype(BF16)
    v3.wait_recv()
    v_hi, v_lo = split(vfull[0:inner, :], 2)
    vcat[...] = jnp.concatenate([v_hi, v_hi, v_lo], axis=0).astype(BF16)
    pre_bias = vfull[inner : inner + 1, :] + winb[...]

    step = hidden // 4
    for c in range(4):
        where = slice(c * step, (c + 1) * step)
        pre = dot(pcat, vcat[:, where], TN) + pre_bias[:, where]
        sig = jax.nn.sigmoid(pre)
        hact[:, where] = (pre * sig).astype(BF16)
        hslope[:, where] = sig * (1.0 + pre * (1.0 - sig))
    relay("x", "b2", (("y", "b2"), ("z", "b2")))
    relay("y", "a", (("z", "e1"),))
    relay("z", "a", (("y", "e2"),))
    target = targ[...].astype(F32)
    unit_target = target * lax.rsqrt(jnp.sum(target * target, axis=1, keepdims=True) + EPS_UNIT)
    beside.wait_recv()
    pair_of = me // 2

    def pair_dot(j):
        base = lax.rem(pair_of + j, n // 2) * (2 * share)
        where = pl.ds(pl.multiple_of(base, 2 * share), 2 * share)
        return dot(hact[:, where], pout[where, :])

    bias_out = jnp.concatenate([woutb[i : i + 1, :] for i in range(woutb.shape[0])], axis=1)
    projected = pair_dot(0) + bias_out
    relay("y", "b1")
    relay("z", "b1")
    relay("x", "d")
    relay("y", "b2")
    relay("z", "b2")
    relay("z", "e1")
    relay("y", "e2")
    arrive(relays)
    for j in range(1, n // 2):
        projected = projected + pair_dot(j)
    inv_len = lax.rsqrt(jnp.sum(projected * projected, axis=1, keepdims=True) + EPS_UNIT)
    unit_proj = projected * inv_len
    cosine = jnp.sum(unit_proj * unit_target, axis=1, keepdims=True)
    grad_out = (-inv_len * (unit_target - cosine * unit_proj)).astype(BF16)
    for c in range(4):
        where = slice(c * step, (c + 1) * step)
        back = dot(grad_out, pout[where, :], NT)
        gh_ref[:, where] = (back * hslope[:, where]).astype(BF16)
    two = dot(vcat[inner:, :], gh_ref[...], NT)
    grad_patch = (two[0:inner] + two[inner:]).astype(BF16)

    grid = []
    for v in range(PATCH):
        grid.append(
            sum(
                dot(grad_patch[u * 8 : (u + 1) * 8], pick[u * PATCH + v], NT)
                for u in range(PATCH)
            )
        )
    low_rows = lax.broadcasted_iota(jnp.int32, (8, cells), 0) < LATENT
    both = jnp.where(low_rows, grid[0], grid[1])
    grad_lat = both + pltpu.roll(both, LATENT, 0)
    grad_lat = jnp.where(low_rows, grad_lat, 0.0)
    ghalo[...] = grad_lat
    ghalo_copies = [
        send(ghalo, ghalo_in.at[0], g_send.at[0], g_recv.at[0], following),
        send(ghalo, ghalo_in.at[1], g_send.at[1], g_recv.at[1], prev),
    ]
    wide = dot(pcat[0 : 2 * inner], gh_ref[...])
    a_sum = wide[0:inner] + wide[inner:]
    a_ref[...] = a_sum
    a16[...] = a_sum.astype(BF16)
    a_copies = spread(a16, a_in, a_send, a_recv)
    arrive(ghalo_copies)
    by_row = [below(grad_lat, ghalo_in[1]), grad_lat, above(grad_lat, ghalo_in[0])]
    grad_taps = jnp.concatenate(
        [beside_col(by_row[dy], 1 - dx) for dy in range(3) for dx in range(3)], axis=0
    ).astype(BF16)
    gs_ref[...] = dot(grad_taps, taps, TN)
    conv = dot(grad_taps, act[...])

    def backward(b, carry):
        where = pl.ds(pl.multiple_of(b * area, area), area)
        gs = gs_ref[where, :] * slope[where, :]
        gs_ref[where, :] = gs
        fs[0, pl.ds(b, 1), :] = jnp.sum(gs, axis=0, keepdims=True)
        fs[1, pl.ds(b, 1), :] = jnp.sum(gs * nrm[where, :], axis=0, keepdims=True)
        return carry

    lax.fori_loop(0, images, backward, 0)
    pooled = exact_dot(jnp.concatenate([fs[0] * gain[...], fs[1] * gain[...]], axis=0), pool, 3)
    fg[0] = pooled[0:rows]
    fg[1] = pooled[rows:]
    f_copies = spread(fg, fg_in, f_send, f_recv)
    gain_row = jnp.sum(fs[1], axis=0, keepdims=True)
    bias_row = jnp.sum(fs[0], axis=0, keepdims=True)
    row8 = lax.broadcasted_iota(jnp.int32, (8, channels), 0)
    per = pack.shape[1] // 8
    lanes = pack.shape[2]
    for i in range(5):
        part_i = conv[16 * i : 16 * i + 8]
        if i < 4:
            part_i = part_i + pltpu.roll(conv[16 * i + 8 : 16 * i + 16], LATENT, 0)
        else:
            part_i = jnp.where(row8 == LATENT, gain_row, part_i)
            part_i = jnp.where(row8 == LATENT + 1, bias_row, part_i)
        for c in range(channels // lanes):
            t = 5 * c + i
            pack[t // per, (t % per) * 8 : (t % per + 1) * 8, :] = (
                part_i[:, c * lanes : (c + 1) * lanes]
            )
    for t in range(5 * (channels // lanes), n * per):
        pack[t // per, (t % per) * 8 : (t % per + 1) * 8, :] = jnp.zeros((8, lanes), F32)
    p_copies = []
    for k in range(1, n):
        peer = lax.rem(me + k, n)
        p_copies.append(
            send(pack.at[peer], pack_in.at[k - 1], p_send.at[k - 1], p_recv.at[k - 1], peer)
        )
    arrive(a_copies)
    a_all = a_ref[...] + sum(a_in[k].astype(F32) for k in range(n - 1))
    emb[...] = exact_dot(a_all, win[...], 2, NT).astype(BF16)
    q_copies = across_batch(emb, emb_in, e_send, e_recv)
    arrive(p_copies)
    piece[...] = (pack[me] + sum(pack_in[k] for k in range(n - 1))).astype(BF16)
    piece_copies = across_batch(piece, piece_in, q_send, q_recv)
    arrive(f_copies)
    totals = [(fg[i] + sum(fg_in[k, i] for k in range(n - 1))) / members for i in range(2)]
    both_means = exact_dot(jnp.concatenate(totals, axis=0), pool, 3, NT)
    stat[2] = both_means[0:rows]
    stat[3] = both_means[rows:]

    def finish(b, carry):
        where = pl.ds(pl.multiple_of(b * area, area), area)
        one = pl.ds(b, 1)
        out[where, :] = (
            stat[1, one, :]
            * (gs_ref[where, :] * gain[...] - stat[2, one, :] - nrm[where, :] * stat[3, one, :])
        ).astype(BF16)
        return carry

    lax.fori_loop(0, images, finish, 0)
    arrive(q_copies)
    whole_emb[me] = ordered(emb, emb_in, group, nb)
    w_copies = []
    for k in range(1, n):
        peer = lax.rem(me + k, n)
        w_copies.append(
            send(whole_emb.at[me], whole_emb.at[me], y_send.at[k - 1], y_recv.at[k - 1], peer)
        )
    arrive(piece_copies)
    whole[me] = ordered(piece, piece_in, group, nb)
    for k in range(1, n):
        peer = lax.rem(me + k, n)
        w_copies.append(send(whole.at[me], whole.at[me], w_send.at[k - 1], w_recv.at[k - 1], peer))
    arrive(w_copies)
    for c in range(channels // lanes):
        at = slice(c * lanes, (c + 1) * lanes)
        for i in range(5):
            t = 5 * c + i
            tile = whole[t // per, (t % per) * 8 : (t % per + 1) * 8, :]
            for side in range(2):
                tap = 2 * i + side
                tile_rows = tile[side * LATENT : (side + 1) * LATENT]
                if tap < 9:
                    start = tap * channels + c * lanes
                    conv_o[:, start : start + lanes] = tile_rows
                else:
                    gain_o[:, at] = tile_rows[0:1]
                    bias_o[:, at] = tile_rows[1:2]
    for k in range(n):
        emb_o[:, k * part : (k + 1) * part] = whole_emb[k]
    for copy in sent:
        copy.wait_send()


def ordered(own, arrived, group, nb):
    total = None
    for g in range(nb):
        slot = lax.rem(group + nb - g, nb)
        value = arrived[jnp.maximum(slot - 1, 0)] if nb > 1 else own[...]
        value = jnp.where(slot == 0, own[...].astype(F32), value.astype(F32))
        total = value if total is None else total + value
    return total


def store(*refs):
    count = (len(refs) - 1) // 2
    sem = refs[-1]
    copies = [
        pltpu.make_async_copy(refs[i], refs[count + i], sem.at[i]) for i in range(count)
    ]
    for copy in copies:
        copy.start()
    for copy in copies:
        copy.wait()


def shards(
    features, norm_gain, norm_bias, conv_weight, embed_weight, embed_bias,
    proj_in, proj_in_bias, proj_out, proj_out_bias, targets,
):
    images, height, across, channels = features.shape
    n = lax.axis_size("rows")
    nb = lax.axis_size("batch")
    lanes = 128
    per = -(-(5 * (channels // lanes)) // n)
    cells = images * height * across
    align = targets.shape[-1]
    tokens = targets.shape[0] * targets.shape[1] * targets.shape[2]
    inner, width = embed_weight.shape
    part, hidden = proj_in.shape
    share = proj_out.shape[0]
    pad_images = -(-images // 8) * 8
    sliced = part % lanes == 0
    embed_bias = embed_bias[None]
    if not sliced:
        me = lax.axis_index("rows")
        embed_weight = lax.dynamic_slice_in_dim(embed_weight, me * part, part, axis=1)
        embed_bias = lax.dynamic_slice_in_dim(embed_bias, me * part, part, axis=1)
    ring = n // 2 - 1
    cols = hidden // 2
    last = max(nb - 1, 1)
    dma = pltpu.SemaphoreType.DMA
    vm = pltpu.VMEM
    results = pl.pallas_call(
        functools.partial(kernel, images, height, across, n, nb, sliced),
        out_shape=(
            vm((cells, channels), BF16),
            vm((LATENT, 9 * channels), F32),
            vm((1, channels), F32),
            vm((1, channels), F32),
            vm((inner, width), F32),
        ),
        in_specs=[pl.BlockSpec(memory_space=pltpu.HBM)] * 11,
        out_specs=[pl.BlockSpec(memory_space=vm)] * 5,
        scratch_shapes=[
            vm((cells, channels), BF16),
            vm((1, channels), F32),
            vm((1, channels), F32),
            vm((LATENT, 9 * channels), BF16),
            vm((inner, part), F32),
            vm((1, part), F32),
            vm((part, hidden), BF16),
            vm((1, hidden), F32),
            vm((align // lanes, lanes), F32),
            vm((tokens, align), BF16),
            vm((2, pad_images, channels), F32),
            vm((2, pad_images, lanes), F32),
            vm((n - 1, 2, pad_images, lanes), F32),
            vm((cells, channels), F32),
            vm((cells, channels), F32),
            vm((cells, channels), BF16),
            vm((cells, channels), F32),
            vm((2, 8, cells), F32),
            vm((2, 8, cells), F32),
            vm((8, cells), F32),
            vm((2, 8, cells), F32),
            vm((inner + 8, hidden), F32),
            vm((inner + 8, cols), F32),
            vm((inner + 8, cols), F32),
            vm((inner + 8, cols), BF16),
            vm((max(ring, 1), inner + 8, cols), BF16),
            vm((inner + 8, hidden), F32),
            vm((3 * inner, hidden), BF16),
            vm((n * share, align), BF16),
            vm((tokens, hidden), BF16),
            vm((tokens, hidden), F32),
            vm((tokens, hidden), BF16),
            vm((inner, hidden), F32),
            vm((inner, hidden), BF16),
            vm((n - 1, inner, hidden), BF16),
            vm((2, pad_images, channels), F32),
            vm((2, pad_images, lanes), F32),
            vm((n - 1, 2, pad_images, lanes), F32),
            vm((4, pad_images, channels), F32),
            vm((n, per * 8, lanes), F32),
            vm((n - 1, per * 8, lanes), F32),
            vm((per * 8, lanes), BF16),
            vm((last, per * 8, lanes), BF16),
            vm((inner, part), BF16),
            vm((last, inner, part), BF16),
            vm((n, per * 8, lanes), F32),
            vm((n, inner, part), F32),
            dma((11,)), dma((n - 1,)), dma((n - 1,)),
            dma((ring + 2,)), dma((ring + 2,)),
            dma((24 * ring + 1,)), dma((24 * ring + 1,)),
            dma((2,)), dma((2,)), dma((2,)), dma((2,)),
            dma((n - 1,)), dma((n - 1,)), dma((n - 1,)), dma((n - 1,)),
            dma((n - 1,)), dma((n - 1,)),
            dma((last,)), dma((last,)), dma((last,)), dma((last,)),
            dma((n - 1,)), dma((n - 1,)), dma((n - 1,)), dma((n - 1,)),
        ],
        compiler_params=pltpu.CompilerParams(
            collective_id=0, has_side_effects=True, vmem_limit_bytes=48 * 1024 * 1024
        ),
        name="alignment_step",
    )(
        features.reshape(cells, channels), norm_gain[None], norm_bias[None], conv_weight,
        embed_weight, embed_bias, proj_in, proj_in_bias[None], proj_out,
        proj_out_bias.reshape(align // lanes, lanes), targets.reshape(tokens, align),
    )
    grad_features, grad_conv, grad_gain, grad_bias, grad_embed = pl.pallas_call(
        store,
        out_shape=tuple(jax.ShapeDtypeStruct(x.shape, x.dtype) for x in results),
        in_specs=[pl.BlockSpec(memory_space=vm)] * 5,
        out_specs=[pl.BlockSpec(memory_space=pltpu.HBM)] * 5,
        scratch_shapes=[dma((5,))],
        compiler_params=pltpu.CompilerParams(vmem_limit_bytes=4 * 1024 * 1024),
        name="store_results",
    )(*results)
    return (
        grad_features.reshape(images, height, across, channels),
        grad_conv, grad_gain[0], grad_bias[0], grad_embed,
    )


def solution(mesh):
    in_specs = (
        P("batch", "rows", None, None), P(), P(), P(), P(), P(),
        P("rows", None), P(), P("rows", None), P(), P("batch", "rows", None, None),
    )
    out_specs = (P("batch", "rows", None, None), P(), P(), P(), P())
    return jax.shard_map(shards, mesh=mesh, in_specs=in_specs, out_specs=out_specs, check_vma=False)
```

time: 73.7 us -> 48.4 us (0.66)
  Pallas kernels: 64.6 us -> 38.4 us
  local copies, waits for them, and re-layouts: 6.62 us -> 8.79 us
  other arithmetic: 1.42 us -> 0 us
    pallas_call x1 -> x2, Pallas kernels: 64.6 us -> 38.4 us  [the longest x1 37.5 us: shards(): pl.pallas_call(functools.partial(kernel, images, height, across, n, nb, s...]
    unnamed x19 -> x22, local copies, waits for them, and re-layouts: 5.26 us -> 8.79 us
    concatenate x2 -> x0, other arithmetic: 1.42 us -> none  [the longest x1 1.4 us: shards(): jnp.concatenate([embed_weight, embed_bias[None], jnp.zeros((7, width), F3...]
    concatenate x2 -> x0, local copies, waits for them, and re-layouts: 0.76 us -> none  [the longest x1 0.68 us: shards(): taps = jnp.concatenate([taps, taps], axis=1).reshape(72, channels)]
where the time goes in v1:
time: 48.4 us; the launch traced here: 47.9 us
  Pallas kernels  38.4 us (79%)
  local copies, waits for them, and re-layouts  8.79 us (18%)
  between operations  0.67 us (1%)
    pallas_call x1, Pallas kernels, shards(): pl.pallas_call(functools.partial(kernel, images, height, across, n, nb, s...  37.5 us
    unnamed x22, local copies, waits for them, and re-layouts  8.79 us

profile of v1, /device:TPU:0, one launch (start us, length us, event | category | flops | bytes accessed | tf_op | source)
XLA Modules:
  0.0 47.9 jit_solution(11496622959466626975)
XLA Ops:
  0.6 0.0 copy-start.6
  0.6 0.0 copy-start.7
  0.7 0.7 %copy-done.6 = f32[2048]{0:T(1024)S(1)} copy-done((f32[2048]{0:T(1024)S(1)}, f32[2048]{0:T(1024)}, u32[]{:S(2)}) %copy-start.6) | copy-done | bytes 8216
  1.3 0.0 copy-done.7
  1.3 0.0 copy-start
  1.3 1.2 %copy-done = bf16[256,2048]{1,0:T(8,128)(2,1)S(1)} copy-done((bf16[256,2048]{1,0:T(8,128)(2,1)S(1)}, bf16[256,2048]{1,0:T(8,128)(2,1)}, u32[]{:S(2)}) %copy-start) | copy-done | bytes 1048600
  2.6 0.0 copy-start.1
  2.6 1.1 %copy-done.1 = bf16[12,2,32,512]{3,2,1,0:T(8,128)(2,1)S(1)} copy-done((bf16[12,2,32,512]{3,2,1,0:T(8,128)(2,1)S(1)}, bf16[12,2,32,512]{3,2,1,0:T(8,128)(2,1)}, u32[]{:S(2)}) %copy-start.1) | copy-done | bytes 786456
  3.7 0.0 copy-start.2
  3.7 1.1 %copy-done.2 = bf16[512,768]{1,0:T(8,128)(2,1)S(1)} copy-done((bf16[512,768]{1,0:T(8,128)(2,1)S(1)}, bf16[512,768]{1,0:T(8,128)(2,1)}, u32[]{:S(2)}) %copy-start.2) | copy-done | bytes 786456
  4.8 0.0 copy-start.3
  4.8 1.0 %copy-done.3 = bf16[12,1,16,768]{3,2,1,0:T(8,128)(2,1)S(1)} copy-done((bf16[12,1,16,768]{3,2,1,0:T(8,128)(2,1)S(1)}, bf16[12,1,16,768]{3,2,1,0:T(8,128)(2,1)}, u32[]{:S(2)}) %copy-start.3) | copy-done | bytes 294936
  5.8 0.0 copy-start.4
  5.8 0.8 %copy-done.4 = f32[16,1024]{1,0:T(8,128)S(1)} copy-done((f32[16,1024]{1,0:T(8,128)S(1)}, f32[16,1024]{1,0:T(8,128)}, u32[]{:S(2)}) %copy-start.4) | copy-done | bytes 65560
  6.6 0.0 copy-start.5
  6.6 0.8 %copy-done.5 = bf16[4,4608]{1,0:T(4,128)(2,1)S(1)} copy-done((bf16[4,4608]{1,0:T(4,128)(2,1)S(1)}, bf16[4,4608]{1,0:T(4,128)(2,1)}, u32[]{:S(2)}) %copy-start.5) | copy-done | bytes 36888
  7.4 0.0 copy-start.8
  7.4 0.7 %copy-done.8 = f32[768]{0:T(1024)S(1)} copy-done((f32[768]{0:T(1024)S(1)}, f32[768]{0:T(1024)}, u32[]{:S(2)}) %copy-start.8) | copy-done | bytes 3096
  8.1 0.0 copy-start.9
  8.1 0.7 %copy-done.9 = f32[512]{0:T(512)S(1)} copy-done((f32[512]{0:T(512)S(1)}, f32[512]{0:T(512)}, u32[]{:S(2)}) %copy-start.9) | copy-done | bytes 2072
  8.8 0.0 copy-start.10
  8.8 0.7 %copy-done.10 = f32[512]{0:T(512)S(1)} copy-done((f32[512]{0:T(512)S(1)}, f32[512]{0:T(512)}, u32[]{:S(2)}) %copy-start.10) | copy-done | bytes 2072
  9.5 37.5 %alignment_step.1 = (bf16[768,512]{1,0:T(8,128)(2,1)S(1)}, f32[4,4608]{1,0:T(4,128)S(1)}, f32[1,512]{1,0:T(1,128)S(1)}, f32[1,512]{1,0:T(1,128)S(1)}, f32[16,1024]{1,0:T(8,128)S(1)}) custom-call(bf16[768,512]{1,0:T(8,128)(2,1)S(1)} %bitcast.10, f32[1,512]{1,0:T(1,128)S(1)} %bitcast.15, f32[1,512]{1,0:T(1,128)S(1)} %bitcast.16, ...), custom_call_target="tpu_custom_call" | custom-call | tf_op jit(solution)/shard_map/alignment_step/pallas_call | solution.py:561
  46.9 1.0 %store_results.1 = (bf16[768,512]{1,0:T(8,128)(2,1)}, f32[4,4608]{1,0:T(4,128)}, f32[1,512]{1,0:T(1,128)}, f32[1,512]{1,0:T(1,128)}, f32[16,1024]{1,0:T(8,128)}) custom-call(bf16[768,512]{1,0:T(8,128)(2,1)S(1)} %get-tuple-element.15.refs_0_, f32[4,4608]{1,0:T(4,128)S(1)} %get-tuple-element.16.refs_1_, f32[1,512]{1,0:T(1,128)S(1)} %get-tuple-element.17.refs_2_, ...), custom_call_target="tpu_custom_call" | custom-call | tf_op jit(solution)/shard_map/store_results/pallas_call | solution.py:638
Async XLA Ops:
  0.6 0.7 %copy-start.6 = (f32[2048]{0:T(1024)S(1)}, f32[2048]{0:T(1024)}, u32[]{:S(2)}) copy-start(f32[2048]{0:T(1024)} %param.18) | copy-start | bytes 24580
  0.6 0.7 %copy-start.7 = (f32[1024]{0:T(1024)S(1)}, f32[1024]{0:T(1024)}, u32[]{:S(2)}) copy-start(f32[1024]{0:T(1024)} %param.16) | copy-start | bytes 12292
  1.3 1.2 %copy-start = (bf16[256,2048]{1,0:T(8,128)(2,1)S(1)}, bf16[256,2048]{1,0:T(8,128)(2,1)}, u32[]{:S(2)}) copy-start(bf16[256,2048]{1,0:T(8,128)(2,1)} %win_h.1) | copy-start | bytes 3145732
  2.6 1.1 %copy-start.1 = (bf16[12,2,32,512]{3,2,1,0:T(8,128)(2,1)S(1)}, bf16[12,2,32,512]{3,2,1,0:T(8,128)(2,1)}, u32[]{:S(2)}) copy-start(bf16[12,2,32,512]{3,2,1,0:T(8,128)(2,1)} %param.11) | copy-start | bytes 2359300
  3.7 1.1 %copy-start.2 = (bf16[512,768]{1,0:T(8,128)(2,1)S(1)}, bf16[512,768]{1,0:T(8,128)(2,1)}, u32[]{:S(2)}) copy-start(bf16[512,768]{1,0:T(8,128)(2,1)} %wout_h.1) | copy-start | bytes 2359300
  4.8 1.0 %copy-start.3 = (bf16[12,1,16,768]{3,2,1,0:T(8,128)(2,1)S(1)}, bf16[12,1,16,768]{3,2,1,0:T(8,128)(2,1)}, u32[]{:S(2)}) copy-start(bf16[12,1,16,768]{3,2,1,0:T(8,128)(2,1)} %param.21) | copy-start | bytes 884740
  5.8 0.8 %copy-start.4 = (f32[16,1024]{1,0:T(8,128)S(1)}, f32[16,1024]{1,0:T(8,128)}, u32[]{:S(2)}) copy-start(f32[16,1024]{1,0:T(8,128)} %embw_h.1) | copy-start | bytes 196612
  6.6 0.8 %copy-start.5 = (bf16[4,4608]{1,0:T(4,128)(2,1)S(1)}, bf16[4,4608]{1,0:T(4,128)(2,1)}, u32[]{:S(2)}) copy-start(bf16[4,4608]{1,0:T(4,128)(2,1)} %conv_h.1) | copy-start | bytes 110596
  7.4 0.7 %copy-start.8 = (f32[768]{0:T(1024)S(1)}, f32[768]{0:T(1024)}, u32[]{:S(2)}) copy-start(f32[768]{0:T(1024)} %param.20) | copy-start | bytes 9220
  8.1 0.7 %copy-start.9 = (f32[512]{0:T(512)S(1)}, f32[512]{0:T(512)}, u32[]{:S(2)}) copy-start(f32[512]{0:T(512)} %param.12) | copy-start | bytes 6148
  8.8 0.7 %copy-start.10 = (f32[512]{0:T(512)S(1)}, f32[512]{0:T(512)}, u32[]{:S(2)}) copy-start(f32[512]{0:T(512)} %param.13) | copy-start | bytes 6148

commit v2 on v1

--- a/solution.py
+++ b/solution.py
@@ -556,6 +556,7 @@
     ring = n // 2 - 1
     cols = hidden // 2
     last = max(nb - 1, 1)
+    reserve = 2 * cells * channels + 4 * (8 * 9 * channels + 16 * channels + inner * width)
     dma = pltpu.SemaphoreType.DMA
     vm = pltpu.VMEM
     results = pl.pallas_call(
@@ -627,7 +628,7 @@
             dma((n - 1,)), dma((n - 1,)), dma((n - 1,)), dma((n - 1,)),
         ],
         compiler_params=pltpu.CompilerParams(
-            collective_id=0, has_side_effects=True, vmem_limit_bytes=48 * 1024 * 1024
+            collective_id=0, has_side_effects=True, vmem_limit_bytes=67043328 - reserve
         ),
         name="alignment_step",
     )(

time: 48.4 us -> 40.4 us (0.83)
  local copies, waits for them, and re-layouts: 8.79 us -> 0 us
  Pallas kernels: 38.4 us -> 39.6 us
    unnamed x22 -> x0, local copies, waits for them, and re-layouts: 8.79 us -> none
    pallas_call x1, Pallas kernels: 37.5 us -> 38.7 us  [shards(): pl.pallas_call(functools.partial(kernel, images, height, across, n, nb, s...]
where the time goes in v2:
time: 40.4 us; the launch traced here: 40.3 us
  Pallas kernels  39.6 us (98%)
  between operations  0.64 us (2%)
    pallas_call x1, Pallas kernels, shards(): pl.pallas_call(functools.partial(kernel, images, height, across, n, nb, s...  38.7 us
    pallas_call x1, Pallas kernels, shards(): pl.pallas_call(store, out_shape=tuple((jax.ShapeDtypeStruct(x.shape, x.dt...  0.97 us

profile of v2, /device:TPU:0, one launch (start us, length us, event | category | flops | bytes accessed | tf_op | source)
XLA Modules:
  0.0 40.3 jit_solution(70899599004167064)
XLA Ops:
  0.6 38.7 %alignment_step.1 = (bf16[768,512]{1,0:T(8,128)(2,1)S(1)}, f32[4,4608]{1,0:T(4,128)S(1)}, f32[1,512]{1,0:T(1,128)S(1)}, f32[1,512]{1,0:T(1,128)S(1)}, f32[16,1024]{1,0:T(8,128)S(1)}) custom-call(bf16[768,512]{1,0:T(8,128)(2,1)} %bitcast.10, f32[1,512]{1,0:T(1,128)} %bitcast.15, f32[1,512]{1,0:T(1,128)} %bitcast.16, bf16[4,4608]{1,0:T(4,128)(2,1)} %conv_h.1, ...), custom_call_target="tpu_custom_call" | custom-call | tf_op jit(solution)/shard_map/alignment_step/pallas_call | solution.py:562
  39.3 1.0 %store_results.1 = (bf16[768,512]{1,0:T(8,128)(2,1)}, f32[4,4608]{1,0:T(4,128)}, f32[1,512]{1,0:T(1,128)}, f32[1,512]{1,0:T(1,128)}, f32[16,1024]{1,0:T(8,128)}) custom-call(bf16[768,512]{1,0:T(8,128)(2,1)S(1)} %get-tuple-element.15.refs_0_, f32[4,4608]{1,0:T(4,128)S(1)} %get-tuple-element.16.refs_1_, f32[1,512]{1,0:T(1,128)S(1)} %get-tuple-element.17.refs_2_, ...), custom_call_target="tpu_custom_call" | custom-call | tf_op jit(solution)/shard_map/store_results/pallas_call | solution.py:639
